TPU v7x, 32 devices: a whole 2x2x4 slice. The times are simulated.
32 devices in a mesh: row: 8 (over y, x, core), col: 4 (over z).
Axes of the slice: x: 2, y: 2, z: 4, core: 2. Of those that a mesh axis runs over, the one named last changes fastest.
Arguments:
- residual: float32 [2048, 2048], P('row', 'col'), may hold values from -0.15625 to 0.15625
- direction: float32 [2048, 2048], P('row', 'col'), may hold values from -6 to 6
- ground_shift: float32 [1], replicated, may hold values from 1.6937256e-06 to 6.7749024e-06
- previous: float32 [1], replicated, may hold values from 192 to 768
Outputs:
- next_direction: float32 [2048, 2048], P('row', 'col')
- step_ratio: float32 [1], replicated
All inputs are finite; a program needn't handle non-finite values.
Results may differ from a plain program's by a relative error of at most 0.00015.
Values sent between devices are 32-bit elements; how exact they have to be, the bound alone decides.
A program may use at most 64 MiB of HBM per device.

v0:
```python
import jax
import jax.numpy as jnp
from jax import lax
from jax.sharding import PartitionSpec as P

PRECISE = lax.Precision.HIGHEST


def mixing_tables(devices):
    target = jnp.arange(devices, dtype=jnp.int32)[:, None]
    source = jnp.arange(devices, dtype=jnp.int32)[None, :]
    angles = jnp.pi * (target * source % (2 * devices)).astype(jnp.float32) / devices
    parity = jnp.where(source % 2 == 0, 1.0, -1.0).astype(jnp.float32)
    return (jnp.cos(angles), jnp.where(target > 0, jnp.sin(angles), parity))


def local_tables(extent, devices, device_index):
    length = extent * devices
    halfway = extent // 2
    position = jnp.arange(extent, dtype=jnp.int32)[:, None]
    steps_m = jnp.arange(halfway, dtype=jnp.int32)
    second_wave = jnp.where(device_index == 0, devices, 2 * devices - device_index)
    first_waves = 2 * devices * steps_m + device_index
    second_waves = 2 * devices * steps_m + second_wave

    def table_pair(wavenums):
        phases = wavenums[None, :] * (2 * position + 1) % (4 * length)
        angles = jnp.pi * phases.astype(jnp.float32) / (2 * length)
        scaling = jnp.where(wavenums == 0, jnp.sqrt(1.0 / length), jnp.sqrt(2.0 / length)).astype(
            jnp.float32
        )
        return (scaling[None, :] * jnp.cos(angles), scaling[None, :] * jnp.sin(angles))

    cos_one, sin_one = table_pair(first_waves)
    cos_two, sin_two = table_pair(second_waves)
    nonzero = (device_index > 0).astype(jnp.float32)
    tables = (
        cos_one,
        -nonzero * sin_one,
        nonzero * cos_two,
        jnp.where(device_index > 0, sin_two, cos_two),
    )
    return (tables, jnp.concatenate([first_waves, second_waves]))


def spread_forward(mix_cos, mix_sin):

    def combine(pieces):
        source = pieces[0]
        real_part = jnp.einsum("td,dab->tab", mix_cos, source, precision=PRECISE)
        imag_part = jnp.einsum("td,dab->tab", mix_sin, source, precision=PRECISE)
        return (real_part, imag_part)

    return combine


def spread_inverse(mix_cos, mix_sin):

    def combine(pieces):
        real_part = jnp.einsum("td,tab->dab", mix_cos, pieces[0], precision=PRECISE)
        imag_part = jnp.einsum("td,tab->dab", mix_sin, pieces[1], precision=PRECISE)
        return (real_part + imag_part,)

    return combine


def across_columns(arrays, combine):
    devices = lax.axis_size("col")

    def handle(pieces):
        mixed = combine(pieces)
        return lax.all_to_all(mixed, "col", split_axis=0, concat_axis=0, tiled=True)

    shaped = tuple(
        (
            member.reshape((devices, member.shape[0] // devices) + member.shape[1:])
            for member in arrays
        )
    )
    result = handle(lax.all_to_all(shaped, "col", split_axis=0, concat_axis=0, tiled=True))
    return tuple((member.reshape((-1,) + member.shape[2:]) for member in result))


def across_rows(arrays, combine):
    devices = lax.axis_size("row")

    def handle(pieces):
        mixed = combine(pieces)
        return lax.all_to_all(mixed, "row", split_axis=0, concat_axis=0, tiled=True)

    shaped = tuple(
        (
            member.reshape((devices, member.shape[0] // devices) + member.shape[1:])
            for member in arrays
        )
    )
    result = handle(lax.all_to_all(shaped, "row", split_axis=0, concat_axis=0, tiled=True))
    return tuple((member.reshape((-1,) + member.shape[2:]) for member in result))


def body(residual, direction, ground_shift, previous):
    row_count = lax.axis_size("row")
    col_count = lax.axis_size("col")
    row_index = lax.axis_index("row")
    col_index = lax.axis_index("col")
    rows_here = residual.shape[0]
    cols_here = residual.shape[1]
    halfway_rows = rows_here // 2
    halfway_cols = cols_here // 2
    col_tables, col_waves = local_tables(cols_here, col_count, col_index)
    row_tables, row_waves = local_tables(rows_here, row_count, row_index)
    col_cos, col_sin = mixing_tables(col_count)
    row_cos, row_sin = mixing_tables(row_count)
    real_part, imag_part = across_columns((residual,), spread_forward(col_cos, col_sin))
    left_half = jnp.dot(real_part, col_tables[0], precision=PRECISE) + jnp.dot(
        imag_part, col_tables[1], precision=PRECISE
    )
    right_half = jnp.dot(real_part, col_tables[2], precision=PRECISE) + jnp.dot(
        imag_part, col_tables[3], precision=PRECISE
    )
    partial_spectrum = jnp.concatenate([left_half, right_half], axis=1)
    real_part, imag_part = across_rows((partial_spectrum,), spread_forward(row_cos, row_sin))
    upper_half = jnp.dot(row_tables[0].T, real_part, precision=PRECISE) + jnp.dot(
        row_tables[1].T, imag_part, precision=PRECISE
    )
    lower_half = jnp.dot(row_tables[2].T, real_part, precision=PRECISE) + jnp.dot(
        row_tables[3].T, imag_part, precision=PRECISE
    )
    spectrum = jnp.concatenate([upper_half, lower_half], axis=0)
    row_total = rows_here * row_count
    col_total = cols_here * col_count
    row_sine = jnp.sin(jnp.pi * row_waves.astype(jnp.float32) / (2 * row_total))
    col_sine = jnp.sin(jnp.pi * col_waves.astype(jnp.float32) / (2 * col_total))
    eigenvalue = 4.0 * (row_sine * row_sine)[:, None] + 4.0 * (col_sine * col_sine)[None, :]
    weight = 1.0 / (eigenvalue + ground_shift[0])
    scaled = weight * spectrum
    upper_half = scaled[:halfway_rows]
    lower_half = scaled[halfway_rows:]
    back_real = jnp.dot(row_tables[0], upper_half, precision=PRECISE) + jnp.dot(
        row_tables[2], lower_half, precision=PRECISE
    )
    back_imag = jnp.dot(row_tables[1], upper_half, precision=PRECISE) + jnp.dot(
        row_tables[3], lower_half, precision=PRECISE
    )
    partial_field = across_rows((back_real, back_imag), spread_inverse(row_cos, row_sin))[0]
    left_half = partial_field[:, :halfway_cols]
    right_half = partial_field[:, halfway_cols:]
    back_real = jnp.dot(left_half, col_tables[0].T, precision=PRECISE) + jnp.dot(
        right_half, col_tables[2].T, precision=PRECISE
    )
    back_imag = jnp.dot(left_half, col_tables[1].T, precision=PRECISE) + jnp.dot(
        right_half, col_tables[3].T, precision=PRECISE
    )
    precond = across_columns((back_real, back_imag), spread_inverse(col_cos, col_sin))[0]
    local_inner = jnp.sum(spectrum * scaled)
    inner_total = lax.psum(local_inner, ("row", "col"))
    step_ratio = inner_total / previous[0]
    return (precond + step_ratio * direction, jnp.reshape(step_ratio, (1,)))


def solution(mesh):
    return jax.shard_map(
        body,
        mesh=mesh,
        in_specs=(P("row", "col"), P("row", "col"), P(), P()),
        out_specs=(P("row", "col"), P()),
        check_vma=False,
    )
```

profile of v0, /device:TPU:0, one launch (start us, length us, event | category | flops | bytes accessed | tf_op | source)
XLA Modules:
  0.0 244.6 jit_solution(7516557142116567969)
XLA Ops:
  0.6 20.8 %all_to_all.60 = f32[4,64,512]{2,1,0:T(8,128)S(1)} all-to-all(f32[4,64,512]{2,1,0:T(8,128)} %bitcast.54), channel_id=1, replica_groups=mesh['row'=8,'col'=4] {'col'}, dimensions={0} | all-to-all | bytes 1048576 | tf_op jit(solution)/shard_map/all_to_all | solution.py:80
  21.5 1.5 fusion.21
  23.0 1.0 copy.34
  24.0 3.5 %all-to-all-start.1 = ((f32[4,64,512]{2,1,0:T(8,128)}), f32[4,64,512]{2,1,0:T(8,128)S(1)}, u32[]{:S(2)}, u32[]{:S(2)}) async-start(f32[4,64,512]{2,1,0:T(8,128)} %copy.34), calls=%async_computation.1 | async-start | bytes 1048576 | tf_op jit(solution)/shard_map/all_to_all | solution.py:72
  27.5 1.5 fusion.19
  29.1 1.0 copy.37
  30.0 11.1 %all-to-all-done.1 = f32[4,64,512]{2,1,0:T(8,128)S(1)} async-done(((f32[4,64,512]{2,1,0:T(8,128)}), f32[4,64,512]{2,1,0:T(8,128)S(1)}, u32[]{:S(2)}, u32[]{:S(2)}) %all-to-all-start.1) | async-done | bytes 524320 | tf_op jit(solution)/shard_map/all_to_all | solution.py:72
  41.1 3.6 %all-to-all-start.2 = ((f32[4,64,512]{2,1,0:T(8,128)}), f32[4,64,512]{2,1,0:T(8,128)S(1)}, u32[]{:S(2)}, u32[]{:S(2)}) async-start(f32[4,64,512]{2,1,0:T(8,128)} %copy.37), calls=%async_computation.2 | async-start | bytes 1048576 | tf_op jit(solution)/shard_map/all_to_all | solution.py:72
  44.8 3.0 %fusion.25 = f32[256,256]{0,1:T(8,128)S(1)} fusion(f32[256,512]{1,0:T(8,128)S(1)} %bitcast.55, f32[256]{0:T(256)S(1)} %compare_select_fusion.2, f32[]{:T(128)S(6)} %convert_element_type.56, s32[256]{0:T(256)S(1)} %get-tuple-element.4, s32[512]{0:T(512)S(1)} %multiply_add_fusion), kind=kOutput, calls=%fused_computation.53 | convolution fusion | flops 404750336 | bytes 790532 | tf_op jit(solution)/shard_map/dot_general | solution.py:118
  47.8 2.9 %fusion.18 = f32[256,256]{0,1:T(8,128)S(1)} fusion(f32[256,512]{1,0:T(8,128)S(1)} %bitcast.56, s32[512]{0:T(512)S(1)} %multiply_add_fusion, s32[256]{0:T(256)S(1)} %get-tuple-element.5, f32[256]{0:T(256)S(1)} %compare_select_fusion.4), kind=kOutput, calls=%fused_computation.47 | convolution fusion | flops 404619264 | bytes 790528 | tf_op jit(solution)/shard_map/dot_general | solution.py:115
  50.8 7.8 %all-to-all-done.2 = f32[4,64,512]{2,1,0:T(8,128)S(1)} async-done(((f32[4,64,512]{2,1,0:T(8,128)}), f32[4,64,512]{2,1,0:T(8,128)S(1)}, u32[]{:S(2)}, u32[]{:S(2)}) %all-to-all-start.2) | async-done | bytes 524320 | tf_op jit(solution)/shard_map/all_to_all | solution.py:72
  58.6 3.1 %convolution_add_fusion.8 = f32[256,256]{0,1:T(8,128)S(1)} fusion(f32[256,256]{0,1:T(8,128)S(1)} %fusion.25, f32[256,512]{1,0:T(8,128)S(1)} %bitcast.57, f32[256]{0:T(256)S(1)} %compare_select_fusion.2, s32[256]{0:T(256)S(1)} %get-tuple-element.4, s32[512]{0:T(512)S(1)} %multiply_add_fusion, pred[]{:T(512)S(6)} %gt.29), kind=kOutput, calls=%fused_computation.8 | convolution fusion | flops 404946944 | bytes 1052673 | tf_op jit(solution)/shard_map/dot_general | solution.py:118
  61.7 3.2 %convolution_add_fusion.9 = f32[256,256]{0,1:T(8,128)S(1)} fusion(f32[256,256]{0,1:T(8,128)S(1)} %fusion.18, f32[256,512]{1,0:T(8,128)S(1)} %bitcast.58, f32[]{:T(128)S(6)} %neg.6, s32[512]{0:T(512)S(1)} %multiply_add_fusion, s32[256]{0:T(256)S(1)} %get-tuple-element.5, f32[256]{0:T(256)S(1)} %compare_select_fusion.4), kind=kOutput, calls=%fused_computation.9 | convolution fusion | flops 404815872 | bytes 1052676 | tf_op jit(solution)/shard_map/dot_general | solution.py:115
  65.0 1.0 copy.38
  66.0 3.7 %all-to-all-start.3 = ((f32[8,32,512]{2,1,0:T(8,128)}), f32[8,32,512]{2,1,0:T(8,128)S(1)}, u32[]{:S(2)}, u32[]{:S(2)}) async-start(f32[8,32,512]{2,1,0:T(8,128)} %bitcast.9), calls=%async_computation.3 | async-start | bytes 1048576 | tf_op jit(solution)/shard_map/all_to_all | solution.py:97
  70.5 9.0 %all-to-all-done.3 = f32[8,32,512]{2,1,0:T(8,128)S(1)} async-done(((f32[8,32,512]{2,1,0:T(8,128)}), f32[8,32,512]{2,1,0:T(8,128)S(1)}, u32[]{:S(2)}, u32[]{:S(2)}) %all-to-all-start.3) | async-done | bytes 524320 | tf_op jit(solution)/shard_map/all_to_all | solution.py:97
  80.3 1.1 copy.41
  81.4 3.5 %all-to-all-start.4 = ((f32[8,32,512]{2,1,0:T(8,128)}), f32[8,32,512]{2,1,0:T(8,128)S(1)}, u32[]{:S(2)}, u32[]{:S(2)}) async-start(f32[8,32,512]{2,1,0:T(8,128)} %copy.41), calls=%async_computation.4 | async-start | bytes 1048576 | tf_op jit(solution)/shard_map/all_to_all | solution.py:89
  85.9 1.1 copy.44
  87.0 7.6 %all-to-all-done.4 = f32[8,32,512]{2,1,0:T(8,128)S(1)} async-done(((f32[8,32,512]{2,1,0:T(8,128)}), f32[8,32,512]{2,1,0:T(8,128)S(1)}, u32[]{:S(2)}, u32[]{:S(2)}) %all-to-all-start.4) | async-done | bytes 524320 | tf_op jit(solution)/shard_map/all_to_all | solution.py:89
  94.6 3.5 %all-to-all-start.5 = ((f32[8,32,512]{2,1,0:T(8,128)}), f32[8,32,512]{2,1,0:T(8,128)S(1)}, u32[]{:S(2)}, u32[]{:S(2)}) async-start(f32[8,32,512]{2,1,0:T(8,128)} %copy.44), calls=%async_computation.5 | async-start | bytes 1048576 | tf_op jit(solution)/shard_map/all_to_all | solution.py:89
  98.1 1.0 fusion.68
  99.1 1.0 fusion.66
  100.1 7.6 %all-to-all-done.5 = f32[8,32,512]{2,1,0:T(8,128)S(1)} async-done(((f32[8,32,512]{2,1,0:T(8,128)}), f32[8,32,512]{2,1,0:T(8,128)S(1)}, u32[]{:S(2)}, u32[]{:S(2)}) %all-to-all-start.5) | async-done | bytes 524320 | tf_op jit(solution)/shard_map/all_to_all | solution.py:89
  107.7 1.0 convolution_add_fusion.6
  108.8 1.0 convolution_add_fusion.7
  110.7 1.1 fusion.57
  111.8 1.9 convolution_add_fusion.3
  113.7 3.5 %all-to-all-start.6 = ((f32[8,32,512]{2,1,0:T(8,128)}), f32[8,32,512]{2,1,0:T(8,128)S(1)}, u32[]{:S(2)}, u32[]{:S(2)}) async-start(f32[8,32,512]{2,1,0:T(8,128)} %bitcast.13), calls=%async_computation.6 | async-start | bytes 1048576 | tf_op jit(solution)/shard_map/all_to_all | solution.py:97
  117.2 1.1 fusion.55
  118.4 2.0 convolution_add_fusion.2
  120.3 6.6 %all-to-all-done.6 = f32[8,32,512]{2,1,0:T(8,128)S(1)} async-done(((f32[8,32,512]{2,1,0:T(8,128)}), f32[8,32,512]{2,1,0:T(8,128)S(1)}, u32[]{:S(2)}, u32[]{:S(2)}) %all-to-all-start.6) | async-done | bytes 524320 | tf_op jit(solution)/shard_map/all_to_all | solution.py:97
  126.9 3.9 %all-to-all-start.7 = ((f32[8,32,512]{2,1,0:T(8,128)}), f32[8,32,512]{2,1,0:T(8,128)S(1)}, u32[]{:S(2)}, u32[]{:S(2)}) async-start(f32[8,32,512]{2,1,0:T(8,128)} %bitcast.15), calls=%async_computation.7 | async-start | bytes 1048576 | tf_op jit(solution)/shard_map/all_to_all | solution.py:97
  131.6 8.8 %all-to-all-done.7 = f32[8,32,512]{2,1,0:T(8,128)S(1)} async-done(((f32[8,32,512]{2,1,0:T(8,128)}), f32[8,32,512]{2,1,0:T(8,128)S(1)}, u32[]{:S(2)}, u32[]{:S(2)}) %all-to-all-start.7) | async-done | bytes 524320 | tf_op jit(solution)/shard_map/all_to_all | solution.py:97
  141.6 12.1 %all_to_all.61 = f32[8,32,512]{2,1,0:T(8,128)S(1)} all-to-all(f32[8,32,512]{2,1,0:T(8,128)S(1)} %copy.47), channel_id=1, replica_groups=mesh['row'=8,'col'=4] {'row'}, dimensions={0} | all-to-all | bytes 1048576 | tf_op jit(solution)/shard_map/all_to_all | solution.py:89
  153.7 2.6 %fusion.17 = f32[256,512]{1,0:T(8,128)S(1)} fusion(s32[512]{0:T(512)S(1)} %multiply_add_fusion, s32[256]{0:T(256)S(1)} %get-tuple-element.5, f32[256]{0:T(256)S(1)} %compare_select_fusion.4, f32[256,512]{1,0:T(8,128)S(1)} %bitcast.59), kind=kOutput, calls=%fused_computation.46 | convolution fusion | flops 404619264 | bytes 790528 | tf_op jit(solution)/shard_map/dot_general | solution.py:148
  156.3 3.6 %convolution_add_fusion.5 = f32[256,512]{1,0:T(8,128)} fusion(f32[256,512]{1,0:T(8,128)S(1)} %fusion.17, f32[256]{0:T(256)S(1)} %compare_select_fusion.2, f32[]{:T(128)S(6)} %convert_element_type.56, s32[256]{0:T(256)S(1)} %get-tuple-element.4, s32[512]{0:T(512)S(1)} %multiply_add_fusion, f32[256,512]{1,0:T(8,128)S(1)} %bitcast.60), kind=kOutput, calls=%fused_computation.5 | convolution fusion | flops 404881408 | bytes 1314820 | tf_op jit(solution)/shard_map/dot_general | solution.py:148
  159.9 3.5 %all-to-all-start.9 = ((f32[4,64,512]{2,1,0:T(8,128)}), f32[4,64,512]{2,1,0:T(8,128)S(1)}, u32[]{:S(2)}, u32[]{:S(2)}) async-start(f32[4,64,512]{2,1,0:T(8,128)} %bitcast.17), calls=%async_computation.9 | async-start | bytes 1048576 | tf_op jit(solution)/shard_map/all_to_all | solution.py:80
  163.4 2.6 %fusion.23 = f32[256,512]{1,0:T(8,128)S(1)} fusion(f32[]{:T(128)S(6)} %neg.6, s32[512]{0:T(512)S(1)} %multiply_add_fusion, s32[256]{0:T(256)S(1)} %get-tuple-element.5, f32[256]{0:T(256)S(1)} %compare_select_fusion.4, f32[256,512]{1,0:T(8,128)S(1)} %bitcast.61), kind=kOutput, calls=%fused_computation.52 | convolution fusion | flops 404750336 | bytes 790532 | tf_op jit(solution)/shard_map/dot_general | solution.py:151
  166.0 3.8 %convolution_add_fusion.4 = f32[256,512]{1,0:T(8,128)} fusion(f32[256,512]{1,0:T(8,128)S(1)} %fusion.23, f32[256]{0:T(256)S(1)} %compare_select_fusion.2, s32[256]{0:T(256)S(1)} %get-tuple-element.4, s32[512]{0:T(512)S(1)} %multiply_add_fusion, pred[]{:T(512)S(6)} %gt.29, f32[256,512]{1,0:T(8,128)S(1)} %bitcast.62), kind=kOutput, calls=%fused_computation.4 | convolution fusion | flops 405012480 | bytes 1314817 | tf_op jit(solution)/shard_map/dot_general | solution.py:151
  169.8 7.8 %all-to-all-done.9 = f32[4,64,512]{2,1,0:T(8,128)S(1)} async-done(((f32[4,64,512]{2,1,0:T(8,128)}), f32[4,64,512]{2,1,0:T(8,128)S(1)}, u32[]{:S(2)}, u32[]{:S(2)}) %all-to-all-start.9) | async-done | bytes 524320 | tf_op jit(solution)/shard_map/all_to_all | solution.py:80
  177.6 3.6 %all-to-all-start.10 = ((f32[4,64,512]{2,1,0:T(8,128)}), f32[4,64,512]{2,1,0:T(8,128)S(1)}, u32[]{:S(2)}, u32[]{:S(2)}) async-start(f32[4,64,512]{2,1,0:T(8,128)} %bitcast.19), calls=%async_computation.10 | async-start | bytes 1048576 | tf_op jit(solution)/shard_map/all_to_all | solution.py:80
  181.2 1.2 fusion.7
  182.5 12.7 %all-to-all-done.10 = f32[4,64,512]{2,1,0:T(8,128)S(1)} async-done(((f32[4,64,512]{2,1,0:T(8,128)}), f32[4,64,512]{2,1,0:T(8,128)S(1)}, u32[]{:S(2)}, u32[]{:S(2)}) %all-to-all-start.10) | async-done | bytes 524320 | tf_op jit(solution)/shard_map/all_to_all | solution.py:80
  195.2 1.3 convolution_add_fusion
  196.5 1.0 copy.50
  197.4 3.6 %all-to-all-start.11 = ((f32[4,64,512]{2,1,0:T(8,128)}), f32[4,64,512]{2,1,0:T(8,128)S(1)}, u32[]{:S(2)}, u32[]{:S(2)}) async-start(f32[4,64,512]{2,1,0:T(8,128)} %copy.50), calls=%async_computation.11 | async-start | bytes 1048576 | tf_op jit(solution)/shard_map/all_to_all | solution.py:72
  201.7 40.0 %psum.7 = f32[]{:T(128)} all-reduce(f32[]{:T(128)} %get-tuple-element.2), channel_id=1, replica_groups=mesh['row'=8,'col'=4] {'row','col'}, use_global_device_ids=true, to_apply=%region_1.2 | all-reduce | flops 1 | bytes 8 | tf_op jit(solution)/shard_map/psum | solution.py:156
  (25 shorter events, 5.7 us)
Async XLA Ops:
  24.0 17.1 %all-to-all-start.1 = ((f32[4,64,512]{2,1,0:T(8,128)}), f32[4,64,512]{2,1,0:T(8,128)S(1)}, u32[]{:S(2)}, u32[]{:S(2)}) async-start(f32[4,64,512]{2,1,0:T(8,128)} %copy.34), calls=%async_computation.1 | async-start | bytes 1048576 | tf_op jit(solution)/shard_map/all_to_all | solution.py:72
  41.1 17.5 %all-to-all-start.2 = ((f32[4,64,512]{2,1,0:T(8,128)}), f32[4,64,512]{2,1,0:T(8,128)S(1)}, u32[]{:S(2)}, u32[]{:S(2)}) async-start(f32[4,64,512]{2,1,0:T(8,128)} %copy.37), calls=%async_computation.2 | async-start | bytes 1048576 | tf_op jit(solution)/shard_map/all_to_all | solution.py:72
  66.0 13.4 %all-to-all-start.3 = ((f32[8,32,512]{2,1,0:T(8,128)}), f32[8,32,512]{2,1,0:T(8,128)S(1)}, u32[]{:S(2)}, u32[]{:S(2)}) async-start(f32[8,32,512]{2,1,0:T(8,128)} %bitcast.9), calls=%async_computation.3 | async-start | bytes 1048576 | tf_op jit(solution)/shard_map/all_to_all | solution.py:97
  81.4 13.2 %all-to-all-start.4 = ((f32[8,32,512]{2,1,0:T(8,128)}), f32[8,32,512]{2,1,0:T(8,128)S(1)}, u32[]{:S(2)}, u32[]{:S(2)}) async-start(f32[8,32,512]{2,1,0:T(8,128)} %copy.41), calls=%async_computation.4 | async-start | bytes 1048576 | tf_op jit(solution)/shard_map/all_to_all | solution.py:89
  94.6 13.1 %all-to-all-start.5 = ((f32[8,32,512]{2,1,0:T(8,128)}), f32[8,32,512]{2,1,0:T(8,128)S(1)}, u32[]{:S(2)}, u32[]{:S(2)}) async-start(f32[8,32,512]{2,1,0:T(8,128)} %copy.44), calls=%async_computation.5 | async-start | bytes 1048576 | tf_op jit(solution)/shard_map/all_to_all | solution.py:89
  113.7 13.2 %all-to-all-start.6 = ((f32[8,32,512]{2,1,0:T(8,128)}), f32[8,32,512]{2,1,0:T(8,128)S(1)}, u32[]{:S(2)}, u32[]{:S(2)}) async-start(f32[8,32,512]{2,1,0:T(8,128)} %bitcast.13), calls=%async_computation.6 | async-start | bytes 1048576 | tf_op jit(solution)/shard_map/all_to_all | solution.py:97
  126.9 13.6 %all-to-all-start.7 = ((f32[8,32,512]{2,1,0:T(8,128)}), f32[8,32,512]{2,1,0:T(8,128)S(1)}, u32[]{:S(2)}, u32[]{:S(2)}) async-start(f32[8,32,512]{2,1,0:T(8,128)} %bitcast.15), calls=%async_computation.7 | async-start | bytes 1048576 | tf_op jit(solution)/shard_map/all_to_all | solution.py:97
  159.9 17.7 %all-to-all-start.9 = ((f32[4,64,512]{2,1,0:T(8,128)}), f32[4,64,512]{2,1,0:T(8,128)S(1)}, u32[]{:S(2)}, u32[]{:S(2)}) async-start(f32[4,64,512]{2,1,0:T(8,128)} %bitcast.17), calls=%async_computation.9 | async-start | bytes 1048576 | tf_op jit(solution)/shard_map/all_to_all | solution.py:80
  177.6 17.6 %all-to-all-start.10 = ((f32[4,64,512]{2,1,0:T(8,128)}), f32[4,64,512]{2,1,0:T(8,128)S(1)}, u32[]{:S(2)}, u32[]{:S(2)}) async-start(f32[4,64,512]{2,1,0:T(8,128)} %bitcast.19), calls=%async_computation.10 | async-start | bytes 1048576 | tf_op jit(solution)/shard_map/all_to_all | solution.py:80
  197.4 45.0 %copy-start = (f32[256,512]{1,0:T(8,128)S(1)}, f32[256,512]{1,0:T(8,128)}, u32[]{:S(2)}) copy-start(f32[256,512]{1,0:T(8,128)} %param.5) | copy-start | bytes 1572868
  197.4 44.9 %all-to-all-start.11 = ((f32[4,64,512]{2,1,0:T(8,128)}), f32[4,64,512]{2,1,0:T(8,128)S(1)}, u32[]{:S(2)}, u32[]{:S(2)}) async-start(f32[4,64,512]{2,1,0:T(8,128)} %copy.50), calls=%async_computation.11 | async-start | bytes 1048576 | tf_op jit(solution)/shard_map/all_to_all | solution.py:72
where the time goes:
time: 249 us; the launch traced here: 245 us
  waiting for transfers between devices  79 us (32%)
  blocking collectives  73 us (29%)
  matrix products  44 us (18%)
  starting transfers between devices  35.9 us (14%)
  local copies, waits for them, and re-layouts  6.4 us (3%)
  between operations  4.28 us (2%)
    psum x1, blocking collectives, body(): inner_total = lax.psum(local_inner, ('row', 'col'))  40 us
    all_to_all x3, waiting for transfers between devices, across_rows(): lax.all_to_all(shaped, 'row', split_axis=0, concat_axis=0, tiled=True)  24.3 us
    all_to_all x1, blocking collectives, across_columns(): lax.all_to_all(shaped, 'col', split_axis=0, concat_axis=0, tiled=True)  20.8 us
    all_to_all x2, waiting for transfers between devices, across_columns(): lax.all_to_all(shaped, 'col', split_axis=0, concat_axis=0, tiled=True)  20.5 us
    all_to_all x3, waiting for transfers between devices, handle(): return lax.all_to_all(mixed, 'col', split_axis=0, concat_axis=0, tiled=True)  18.9 us
    all_to_all x2, waiting for transfers between devices, handle(): return lax.all_to_all(mixed, 'row', split_axis=0, concat_axis=0, tiled=True)  15.2 us
    all_to_all x1, blocking collectives, handle(): return lax.all_to_all(mixed, 'row', split_axis=0, concat_axis=0, tiled=True)  12.1 us
    all_to_all x3, starting transfers between devices, across_rows(): lax.all_to_all(shaped, 'row', split_axis=0, concat_axis=0, tiled=True)  11.1 us
  transfers between devices with their start and end apart: 10, of which 9 were waited for; matrix products, arithmetic and copies ran while one was open for 10% of the time, Pallas kernels for 0%

commit v1 on v0

v1 whole, which is shorter than its diff:
```python
import functools
import math

import jax
import jax.numpy as jnp
import numpy as np
from jax import lax
from jax.experimental import pallas as pl
from jax.experimental.pallas import tpu as pltpu
from jax.sharding import PartitionSpec as P

MESH = pl.DeviceIdType.MESH


def base_tables(extent, devices):
    length = extent * devices
    half = extent // 2
    odd = 2 * np.arange(extent, dtype=np.int64)[:, None] + 1
    steps = 2 * devices * np.arange(half + 1, dtype=np.int64)[None, :]
    coarse = np.pi * (steps * odd % (4 * length)) / (2 * length)
    scale = math.sqrt(2.0 / length)
    cos_a, sin_a = scale * np.cos(coarse), scale * np.sin(coarse)
    lanes = -(-(devices + 1) // 128) * 128
    fine = np.pi * np.arange(lanes, dtype=np.int64)[None, :] * odd / (2 * length)
    coarse_tables = np.stack([cos_a[:, :-1], sin_a[:, :-1], cos_a[:, 1:], sin_a[:, 1:]])
    fine_tables = np.stack([np.cos(fine), np.sin(fine)])
    waves = []
    for t in range(devices):
        second = devices if t == 0 else 2 * devices - t
        waves.append(2 * devices * np.arange(half) + t)
        waves.append(2 * devices * np.arange(half) + second)
    waves = np.concatenate(waves)
    eigen = 4.0 * np.sin(np.pi * waves / (2 * length)) ** 2
    return (
        coarse_tables.astype(np.float32),
        fine_tables.astype(np.float32),
        eigen.astype(np.float32)[None, :],
    )


def mixing(devices):
    target = np.arange(devices)[:, None]
    source = np.arange(devices)[None, :]
    angles = np.pi * (target * source % (2 * devices)) / devices
    parity = np.where(source % 2 == 0, 1.0, -1.0)
    return np.cos(angles), np.where(target > 0, np.sin(angles), parity)


def weighted_sum(coefs, terms):
    total = None
    for coef, term in zip(coefs, terms):
        coef = float(coef)
        if abs(coef) < 1e-12:
            continue
        if abs(coef - 1.0) < 1e-12:
            total = term if total is None else total + term
        elif abs(coef + 1.0) < 1e-12:
            total = -term if total is None else total - term
        else:
            total = coef * term if total is None else total + coef * term
    return total


def split(value):
    high = value.astype(jnp.bfloat16)
    return high, (value - high.astype(jnp.float32)).astype(jnp.bfloat16)


def kernel(
    rows,
    cols,
    residual_ref,
    coarse_ref,
    fine_ref,
    eigen_ref,
    shift_ref,
    previous_ref,
    out_ref,
    ratio_ref,
    out1,
    in1,
    out2,
    in2,
    table_hi,
    table_lo,
    spec,
    field,
    rowsum,
    colsum,
    inner_row,
    inner_col,
    s1,
    r1,
    s2,
    r2,
    s3,
    r3,
    s4,
    r4,
    s5,
    r5,
    s6,
    r6,
):
    me_r = lax.axis_index("row")
    me_c = lax.axis_index("col")
    extent = residual_ref.shape[0]
    width = out1.shape[1]
    half = extent // 2
    total_cols = width * rows * cols
    f32 = jnp.float32
    mix_cos, mix_sin = mixing(rows)

    barrier = pltpu.get_barrier_semaphore()
    for o in range(1, rows):
        pl.semaphore_signal(
            barrier, inc=1, device_id={"row": lax.rem(me_r + o, rows)}, device_id_type=MESH
        )
    for o in range(1, cols):
        pl.semaphore_signal(
            barrier, inc=1, device_id={"col": lax.rem(me_c + o, cols)}, device_id_type=MESH
        )

    def share(axis, me, count, source, landing, send_sems, recv_sems):
        copies = []
        for o in range(1, count):
            to = lax.rem(me + o, count)
            copy = pltpu.make_async_remote_copy(
                src_ref=source(to),
                dst_ref=landing.at[me],
                send_sem=send_sems.at[o - 1],
                recv_sem=recv_sems.at[o - 1],
                device_id={axis: to},
                device_id_type=MESH,
            )
            copy.start()
            copies.append(copy)
        return copies

    for e in range(0, residual_ref.shape[1], 128):
        turned = residual_ref[:, e : e + 128].T
        for i in range(128 // width):
            out1[e // width + i] = turned[i * width : (i + 1) * width]
    pl.semaphore_wait(barrier, rows + cols - 2)
    first = share("row", me_r, rows, lambda to: out1.at[to], in1, s1, r1)
    in1[me_r] = out1[me_r]

    cos_a, sin_a = coarse_ref[0], coarse_ref[1]
    for t in range(rows):
        if t == 0:
            lane = lax.broadcasted_iota(jnp.int32, (extent, half), 1)
            one = jnp.where(lane == 0, math.sqrt(0.5), 1.0) * coarse_ref[0]
            cos_b = fine_ref[0, :, rows : rows + 1]
            sin_b = fine_ref[1, :, rows : rows + 1]
            two = coarse_ref[0] * cos_b - coarse_ref[1] * sin_b
            zero = jnp.zeros_like(one)
            quads = ((one, zero), (zero, two))
        else:
            cos_b = fine_ref[0, :, t : t + 1]
            sin_b = fine_ref[1, :, t : t + 1]
            quads = (
                (
                    coarse_ref[0] * cos_b - coarse_ref[1] * sin_b,
                    coarse_ref[2] * cos_b + coarse_ref[3] * sin_b,
                ),
                (
                    -(coarse_ref[1] * cos_b + coarse_ref[0] * sin_b),
                    coarse_ref[3] * cos_b - coarse_ref[2] * sin_b,
                ),
            )
        for i in range(2):
            for j in range(2):
                high, low = split(quads[i][j])
                at = (t, slice(i * extent, (i + 1) * extent), slice(j * half, (j + 1) * half))
                table_hi[at] = high
                table_lo[at] = low

    alpha = eigen_ref[...] + shift_ref[0]
    h = 0.5 * jnp.sqrt(alpha)
    z = h / (1.0 + jnp.sqrt(1.0 + h * h))
    z2 = z * z
    series = jnp.full_like(z, 1.0 / 23)
    for p in range(21, 0, -2):
        series = series * z2 + 1.0 / p
    theta = 4.0 * z * series
    gain = 0.5 / jnp.sqrt(alpha * (1.0 + 0.25 * alpha))

    def decay(steps):
        return jnp.exp(-theta * steps)

    for copy in first:
        copy.wait_recv()

    place = lax.broadcasted_iota(jnp.int32, (width, extent), 0)
    for t in range(rows):
        lanes = slice(t * extent, (t + 1) * extent)
        pieces = [in1[d] for d in range(rows)]
        real = weighted_sum(mix_cos[t], pieces)
        imag = weighted_sum(mix_sin[t], pieces)
        high, low = split(jnp.concatenate([real, imag], axis=1))
        both = jnp.dot(
            jnp.concatenate([high, low], axis=0), table_hi[t], preferred_element_type=f32
        )
        value = (
            both[:width] + both[width:] + jnp.dot(high, table_lo[t], preferred_element_type=f32)
        )
        spec[:, lanes] = value
        ahead = value
        behind = value
        q = jnp.exp(-theta[:, lanes])
        s = 1
        while s < width:
            ahead = ahead + q * jnp.where(place >= s, pltpu.roll(ahead, s, 0), 0.0)
            behind = behind + q * jnp.where(
                place < width - s, pltpu.roll(behind, width - s, 0), 0.0
            )
            q = q * q
            s *= 2
        field[:, lanes] = ahead + behind - value
        rowsum[me_r, 0:1, lanes] = ahead[width - 1 : width]
        rowsum[me_r, 1:2, lanes] = behind[0:1]
    mine = rowsum.at[me_r]
    second = share("row", me_r, rows, lambda to: mine, rowsum, s2, r2)
    chunk = decay(float(width))
    group = decay(float(width * rows))
    whole = decay(float(total_cols))
    for copy in second:
        copy.wait_recv()

    def carry(sums, count, me, ratio):
        zero = jnp.zeros_like(ratio)
        left, right, at_end, at_start = zero, zero, zero, zero
        for k in range(count):
            a = sums[k, 0:1, :]
            b = sums[count - 1 - k, 1:2, :]
            at_end = ratio * at_end + a
            at_start = ratio * at_start + b
            left = jnp.where(k < me, at_end, left)
            right = jnp.where(count - 1 - k > me, at_start, right)
        return left, right, at_end, at_start

    left_r, right_r, at_end, at_start = carry(rowsum, rows, me_r, chunk)
    colsum[me_c, 0:1, :] = at_end
    colsum[me_c, 1:2, :] = at_start
    mine = colsum.at[me_c]
    third = share("col", me_c, cols, lambda to: mine, colsum, s3, r3)
    up_r = decay((width * me_r).astype(f32))
    down_r = decay((width * (rows - 1 - me_r)).astype(f32))
    up_c = decay((width * rows * me_c).astype(f32))
    down_c = decay((width * rows * (cols - 1 - me_c)).astype(f32))
    for copy in third:
        copy.wait_recv()
    left_c, right_c, at_end, at_start = carry(colsum, cols, me_c, group)
    images = 1.0 / (1.0 - whole * whole)
    left_c = left_c + up_c * ((at_start + whole * at_end) * images)
    right_c = right_c + down_c * ((at_end + whole * at_start) * images)
    left = left_r + up_r * left_c
    right = right_r + down_r * right_c

    fplace = place.astype(f32)
    reals, imags = [], []
    partial = jnp.zeros((1, extent), f32)
    for t in range(rows):
        lanes = slice(t * extent, (t + 1) * extent)
        th = theta[:, lanes]
        value = gain[:, lanes] * (
            field[:, lanes]
            + jnp.exp(-th * (fplace + 1.0)) * left[:, lanes]
            + jnp.exp(-th * (width - fplace)) * right[:, lanes]
        )
        partial = partial + jnp.sum(spec[:, lanes] * value, axis=0, keepdims=True)
        field[:, lanes] = value
    inner_row[me_r] = jnp.broadcast_to(jnp.sum(partial, axis=1, keepdims=True), (8, 128))
    mine = inner_row.at[me_r]
    fourth = share("row", me_r, rows, lambda to: mine, inner_row, s4, r4)
    turn = (((1,), (1,)), ((), ()))
    for t in range(rows):
        lanes = slice(t * extent, (t + 1) * extent)
        high, low = split(field[:, lanes])
        both = lax.dot_general(
            jnp.concatenate([high, low], axis=0), table_hi[t], turn, preferred_element_type=f32
        )
        value = (
            both[:width]
            + both[width:]
            + lax.dot_general(high, table_lo[t], turn, preferred_element_type=f32)
        )
        reals.append(value[:, :extent])
        imags.append(value[:, extent:])
    for d in range(rows):
        out2[d] = weighted_sum(
            list(mix_cos[:, d]) + list(mix_sin[:, d]), reals + imags
        )
    fifth = share("row", me_r, rows, lambda to: out2.at[to], in2, s5, r5)
    in2[me_r] = out2[me_r]
    for copy in fourth:
        copy.wait_recv()
    inner_col[me_c] = jnp.sum(inner_row[...], axis=0)
    mine = inner_col.at[me_c]
    sixth = share("col", me_c, cols, lambda to: mine, inner_col, s6, r6)
    for copy in sixth:
        copy.wait_recv()
    ratio_ref[...] = jnp.sum(inner_col[...], axis=0) / previous_ref[0]
    for copy in fifth:
        copy.wait_recv()
    for e in range(0, out_ref.shape[1], 128):
        turned = jnp.concatenate([in2[e // width + i] for i in range(128 // width)], axis=0)
        out_ref[:, e : e + 128] = turned.T
    for copies in (first, second, third, fourth, fifth, sixth):
        for copy in copies:
            copy.wait_send()


def body(rows, cols, residual, direction, ground_shift, previous):
    extent, here = residual.shape
    width = here // rows
    length = extent * rows
    f32 = jnp.float32
    coarse, fine, eigen = base_tables(extent, rows)
    vmem = pl.BlockSpec(memory_space=pltpu.VMEM)
    smem = pl.BlockSpec(memory_space=pltpu.SMEM)
    dma = pltpu.SemaphoreType.DMA
    per_row, per_col = max(rows - 1, 1), max(cols - 1, 1)
    precond, ratio = pl.pallas_call(
        functools.partial(kernel, rows, cols),
        out_shape=(
            jax.ShapeDtypeStruct((extent, here), f32),
            jax.ShapeDtypeStruct((8, 128), f32),
        ),
        in_specs=[vmem, vmem, vmem, vmem, smem, smem],
        out_specs=(vmem, vmem),
        scratch_shapes=[
            pltpu.VMEM((rows, width, extent), f32),
            pltpu.VMEM((rows, width, extent), f32),
            pltpu.VMEM((rows, width, extent), f32),
            pltpu.VMEM((rows, width, extent), f32),
            pltpu.VMEM((rows, 2 * extent, extent), jnp.bfloat16),
            pltpu.VMEM((rows, 2 * extent, extent), jnp.bfloat16),
            pltpu.VMEM((width, length), f32),
            pltpu.VMEM((width, length), f32),
            pltpu.VMEM((rows, 2, length), f32),
            pltpu.VMEM((cols, 2, length), f32),
            pltpu.VMEM((rows, 8, 128), f32),
            pltpu.VMEM((cols, 8, 128), f32),
            dma((per_row,)),
            dma((per_row,)),
            dma((per_row,)),
            dma((per_row,)),
            dma((per_col,)),
            dma((per_col,)),
            dma((per_row,)),
            dma((per_row,)),
            dma((per_row,)),
            dma((per_row,)),
            dma((per_col,)),
            dma((per_col,)),
        ],
        compiler_params=pltpu.CompilerParams(collective_id=0, has_side_effects=True),
    )(residual, coarse, fine, eigen, ground_shift, previous)
    step_ratio = ratio[0, :1]
    return precond + step_ratio * direction, step_ratio


def solution(mesh):
    return jax.shard_map(
        functools.partial(body, mesh.shape["row"], mesh.shape["col"]),
        mesh=mesh,
        in_specs=(P("row", "col"), P("row", "col"), P(), P()),
        out_specs=(P("row", "col"), P()),
        check_vma=False,
    )
```

time: 249 us -> 38.5 us (0.15); the launches traced: 245 us -> 38.2 us
  waiting for transfers between devices: 79 us -> 0 us
  blocking collectives: 73 us -> 0 us
  matrix products: 44 us -> 0 us
  starting transfers between devices: 35.9 us -> 0 us
  Pallas kernels: 0 us -> 32.4 us
  local copies, waits for them, and re-layouts: 6.4 us -> 1.2 us
    all_to_all x10 -> x0, waiting for transfers between devices: 79 us -> none  [the longest x3 24.3 us: across_rows(): lax.all_to_all(shaped, 'row', split_axis=0, concat_axis=0, tiled=True)]
    dot_general x24 -> x0, matrix products: 44 us -> none  [the longest x1 3.79 us: body(): jnp.dot(right_half, col_tables[3].T, precision=PRECISE)]
    psum x1 -> x0, blocking collectives: 40 us -> none  [body(): inner_total = lax.psum(local_inner, ('row', 'col'))]
    all_to_all x10 -> x0, starting transfers between devices: 35.9 us -> none  [the longest x3 11.1 us: across_rows(): lax.all_to_all(shaped, 'row', split_axis=0, concat_axis=0, tiled=True)]
    all_to_all x2 -> x0, blocking collectives: 33 us -> none  [the longest x1 20.8 us: across_columns(): lax.all_to_all(shaped, 'col', split_axis=0, concat_axis=0, tiled=True)]
    pallas_call x0 -> x1, Pallas kernels: none -> 32.4 us  [body(): pl.pallas_call(functools.partial(kernel, rows, cols), out_shape=(jax.Shap...]
    dot_general x4 -> x0, local copies, waits for them, and re-layouts: 4.14 us -> none  [the longest x2 2.08 us: combine(): imag_part = jnp.einsum('td,dab->tab', mix_sin, source, precision=PRECISE)]
  transfers between devices with their start and end apart: 10 -> 0, of which waited for: 9 -> 0; matrix products, arithmetic and copies ran while one was open for 10% -> 0% of each run, Pallas kernels for 0% -> 0%
where the time goes in v1:
time: 38.5 us; the launch traced here: 38.2 us
  Pallas kernels  32.4 us (84%)
  other arithmetic  2.57 us (7%)
  between operations  1.94 us (5%)
  local copies, waits for them, and re-layouts  1.2 us (3%)
    pallas_call x1, Pallas kernels, body(): pl.pallas_call(functools.partial(kernel, rows, cols), out_shape=(jax.Shap...  32.4 us
    add x1, other arithmetic, body(): return (precond + step_ratio * direction, step_ratio)  2.57 us
    slice x1, local copies, waits for them, and re-layouts, body(): step_ratio = ratio[0, :1]  1.19 us

profile of v1, /device:TPU:0, one launch (start us, length us, event | category | flops | bytes accessed | tf_op | source)
XLA Modules:
  0.0 38.2 jit_solution(5623109591346729589)
XLA Ops:
  1.9 0.0 copy-start
  1.9 32.4 %shard_map.86 = (f32[256,512]{1,0:T(8,128)}, f32[8,128]{1,0:T(8,128)}) custom-call(f32[256,512]{1,0:T(8,128)} %residual_ref.1, f32[4,256,128]{2,1,0:T(8,128)} %constant.6.clone.coarse_ref, f32[2,256,128]{2,1,0:T(8,128)} %constant.7.clone.fine_ref, f32[1,2048]{1,0:T(1,128)} %constant.8.clone.eigen_ref, f32[1]{0:T(128)S(6)} %copy.9.shift_ref, ...), custom_call_target="tpu_custom_call" | custom-call | tf_op jit(solution)/shard_map/pallas_call | solution.py:324
  34.4 1.2 %slice.3 = f32[1,1]{1,0:T(1,128)} slice(f32[8,128]{1,0:T(8,128)} %get-tuple-element.5), slice={[0:1], [0:1]} | slice | bytes 8 | tf_op jit(solution)/shard_map/slice | solution.py:360
  35.6 0.0 copy-done
  35.6 2.6 %multiply_add_fusion = f32[256,512]{1,0:T(8,128)} fusion(f32[256,512]{1,0:T(8,128)} %get-tuple-element.4, f32[256,512]{1,0:T(8,128)S(1)} %copy-done, f32[]{:T(128)} %bitcast), kind=kLoop, calls=%fused_computation | loop fusion | flops 262144 | bytes 1572868 | tf_op jit(solution)/shard_map/add | solution.py:361
Async XLA Ops:
  1.9 33.7 %copy-start = (f32[256,512]{1,0:T(8,128)S(1)}, f32[256,512]{1,0:T(8,128)}, u32[]{:S(2)}) copy-start(f32[256,512]{1,0:T(8,128)} %param.8) | copy-start | bytes 1572868

commit v2 on v1

v2 whole, which is shorter than its diff:
```python
import functools
import math

import jax
import jax.numpy as jnp
import numpy as np
from jax import lax
from jax.experimental import pallas as pl
from jax.experimental.pallas import tpu as pltpu
from jax.sharding import PartitionSpec as P

MESH = pl.DeviceIdType.MESH


def base_tables(extent, devices):
    length = extent * devices
    half = extent // 2
    odd = 2 * np.arange(extent, dtype=np.int64)[:, None] + 1
    steps = 2 * devices * np.arange(half + 1, dtype=np.int64)[None, :]
    coarse = np.pi * (steps * odd % (4 * length)) / (2 * length)
    scale = math.sqrt(2.0 / length)
    cos_a, sin_a = scale * np.cos(coarse), scale * np.sin(coarse)
    lanes = -(-(devices + 1) // 128) * 128
    fine = np.pi * np.arange(lanes, dtype=np.int64)[None, :] * odd / (2 * length)
    coarse_tables = np.stack([cos_a[:, :-1], sin_a[:, :-1], cos_a[:, 1:], sin_a[:, 1:]])
    fine_tables = np.stack([np.cos(fine), np.sin(fine)])
    waves = []
    for t in range(devices):
        second = devices if t == 0 else 2 * devices - t
        waves.append(2 * devices * np.arange(half) + t)
        waves.append(2 * devices * np.arange(half) + second)
    waves = np.concatenate(waves)
    eigen = 4.0 * np.sin(np.pi * waves / (2 * length)) ** 2
    return (
        coarse_tables.astype(np.float32),
        fine_tables.astype(np.float32),
        eigen.astype(np.float32)[None, :],
    )


def mixing(devices):
    target = np.arange(devices)[:, None]
    source = np.arange(devices)[None, :]
    angles = np.pi * (target * source % (2 * devices)) / devices
    parity = np.where(source % 2 == 0, 1.0, -1.0)
    return np.cos(angles), np.where(target > 0, np.sin(angles), parity)


def weighted_sum(coefs, terms):
    total = None
    for coef, term in zip(coefs, terms):
        coef = float(coef)
        if abs(coef) < 1e-12:
            continue
        if abs(coef - 1.0) < 1e-12:
            total = term if total is None else total + term
        elif abs(coef + 1.0) < 1e-12:
            total = -term if total is None else total - term
        else:
            total = coef * term if total is None else total + coef * term
    return total


def split(value):
    high = value.astype(jnp.bfloat16)
    return high, (value - high.astype(jnp.float32)).astype(jnp.bfloat16)


def kernel(
    rows,
    cols,
    residual_hbm,
    direction_hbm,
    coarse_hbm,
    fine_hbm,
    eigen_ref,
    shift_ref,
    previous_ref,
    out_hbm,
    ratio_ref,
    residual_ref,
    direction_ref,
    coarse_ref,
    fine_ref,
    out_ref,
    load_sems,
    store_sems,
    out1,
    in1,
    out2,
    in2,
    table_hi,
    table_lo,
    field,
    from_left,
    from_right,
    own_hi,
    own_lo,
    carried_hi,
    carried_lo,
    rowsum,
    colsum,
    carry,
    s1,
    r1,
    s2,
    r2,
    s3,
    r3,
    s5,
    r5,
):
    me_r = lax.axis_index("row")
    me_c = lax.axis_index("col")
    extent = residual_ref.shape[0]
    width = out1.shape[1]
    half = extent // 2
    total_cols = width * rows * cols
    f32 = jnp.float32
    mix_cos, mix_sin = mixing(rows)

    barrier = pltpu.get_barrier_semaphore()
    for o in range(1, rows):
        pl.semaphore_signal(
            barrier, inc=1, device_id={"row": lax.rem(me_r + o, rows)}, device_id_type=MESH
        )
    for o in range(1, cols):
        pl.semaphore_signal(
            barrier, inc=1, device_id={"col": lax.rem(me_c + o, cols)}, device_id_type=MESH
        )

    loads = []
    for i, (source, landing) in enumerate(
        (
            (residual_hbm, residual_ref),
            (coarse_hbm, coarse_ref),
            (fine_hbm, fine_ref),
            (direction_hbm, direction_ref),
        )
    ):
        copy = pltpu.make_async_copy(source, landing, load_sems.at[i])
        copy.start()
        loads.append(copy)

    def share(axis, me, count, source, landing, send_sems, recv_sems):
        copies = []
        for o in range(1, count):
            to = lax.rem(me + o, count)
            copy = pltpu.make_async_remote_copy(
                src_ref=source(to),
                dst_ref=landing.at[me],
                send_sem=send_sems.at[o - 1],
                recv_sem=recv_sems.at[o - 1],
                device_id={axis: to},
                device_id_type=MESH,
            )
            copy.start()
            copies.append(copy)
        return copies

    loads[0].wait()
    for e in range(0, residual_ref.shape[1], 128):
        turned = residual_ref[:, e : e + 128].T
        for i in range(128 // width):
            out1[e // width + i] = turned[i * width : (i + 1) * width]
    pl.semaphore_wait(barrier, rows + cols - 2)
    first = share("row", me_r, rows, lambda to: out1.at[to], in1, s1, r1)
    in1[me_r] = out1[me_r]

    loads[1].wait()
    loads[2].wait()

    def quadrants(t):
        if t == 0:
            lane = lax.broadcasted_iota(jnp.int32, (extent, half), 1)
            one = jnp.where(lane == 0, math.sqrt(0.5), 1.0) * coarse_ref[0]
            cos_b = fine_ref[0, :, rows : rows + 1]
            sin_b = fine_ref[1, :, rows : rows + 1]
            two = coarse_ref[0] * cos_b - coarse_ref[1] * sin_b
            zero = jnp.zeros_like(one)
            return ((one, zero), (zero, two))
        cos_b = fine_ref[0, :, t : t + 1]
        sin_b = fine_ref[1, :, t : t + 1]
        return (
            (
                coarse_ref[0] * cos_b - coarse_ref[1] * sin_b,
                coarse_ref[2] * cos_b + coarse_ref[3] * sin_b,
            ),
            (
                -(coarse_ref[1] * cos_b + coarse_ref[0] * sin_b),
                coarse_ref[3] * cos_b - coarse_ref[2] * sin_b,
            ),
        )

    for t in range(rows):
        quads = quadrants(t)
        for i in range(2):
            for j in range(2):
                high, low = split(quads[i][j])
                at = (t, slice(i * extent, (i + 1) * extent), slice(j * half, (j + 1) * half))
                table_hi[at] = high
                table_lo[at] = low

    alpha = eigen_ref[...] + shift_ref[...]
    h = 0.5 * jnp.sqrt(alpha)
    z = h / (1.0 + jnp.sqrt(1.0 + h * h))
    z2 = z * z
    series = jnp.full_like(z, 1.0 / 23)
    for p in range(21, 0, -2):
        series = series * z2 + 1.0 / p
    theta = 4.0 * z * series
    gain = 0.5 / jnp.sqrt(alpha * (1.0 + 0.25 * alpha))

    q_one = jnp.exp(-theta)
    place = lax.broadcasted_iota(jnp.int32, (width, extent), 0)
    fplace = place.astype(f32)
    for t in range(rows):
        lanes = slice(t * extent, (t + 1) * extent)
        from_left[:, lanes] = gain[:, lanes] * jnp.exp(-theta[:, lanes] * (fplace + 1.0))
        from_right[:, lanes] = gain[:, lanes] * jnp.exp(-theta[:, lanes] * (width - fplace))
    chunk = jnp.exp(-theta * float(width))
    group = jnp.exp(-theta * float(width * rows))
    whole = jnp.exp(-theta * float(total_cols))

    for copy in first:
        copy.wait_recv()

    length = rows * extent
    partial = jnp.zeros((1, extent), f32)
    for t in range(rows):
        lanes = slice(t * extent, (t + 1) * extent)
        pieces = [in1[d] for d in range(rows)]
        real = weighted_sum(mix_cos[t], pieces)
        imag = weighted_sum(mix_sin[t], pieces)
        high, low = split(jnp.concatenate([real, imag], axis=1))
        both = jnp.dot(
            jnp.concatenate([high, low], axis=0), table_hi[t], preferred_element_type=f32
        )
        value = (
            both[:width] + both[width:] + jnp.dot(high, table_lo[t], preferred_element_type=f32)
        )
        ahead = value
        behind = value
        q = q_one[:, lanes]
        s = 1
        while s < width:
            ahead = ahead + q * jnp.where(place >= s, pltpu.roll(ahead, s, 0), 0.0)
            behind = behind + q * jnp.where(
                place < width - s, pltpu.roll(behind, width - s, 0), 0.0
            )
            q = q * q
            s *= 2
        solved = gain[:, lanes] * (ahead + behind - value)
        partial = partial + jnp.sum(value * solved, axis=0, keepdims=True)
        field[:, lanes] = solved
        rowsum[me_r, 0:1, lanes] = ahead[width - 1 : width]
        rowsum[me_r, 1:2, lanes] = behind[0:1]

    def fold(row):
        return sum(row[:, i : i + 128] for i in range(0, row.shape[1], 128))

    spare = slice(length, length + 128)
    rowsum[me_r, 0:1, spare] = fold(partial)
    rowsum[me_r, 1:2, spare] = jnp.zeros((1, 128), f32)
    mine = rowsum.at[me_r]
    second = share("row", me_r, rows, lambda to: mine, rowsum, s2, r2)

    turn = (((1,), (1,)), ((), ()))
    reals, imags = [], []
    for t in range(rows):
        lanes = slice(t * extent, (t + 1) * extent)
        high, low = split(field[:, lanes])
        both = lax.dot_general(
            jnp.concatenate([high, low], axis=0), table_hi[t], turn, preferred_element_type=f32
        )
        value = (
            both[:width]
            + both[width:]
            + lax.dot_general(high, table_lo[t], turn, preferred_element_type=f32)
        )
        reals.append(value[:, :extent])
        imags.append(value[:, extent:])
    for d in range(rows):
        out2[d] = weighted_sum(list(mix_cos[:, d]) + list(mix_sin[:, d]), reals + imags)
    fifth = share("row", me_r, rows, lambda to: out2.at[to], in2, s5, r5)
    in2[me_r] = out2[me_r]
    for copy in second:
        copy.wait_recv()

    def carries(sums, count, ratio):
        left, right = [jnp.zeros_like(ratio)], [jnp.zeros_like(ratio)]
        for k in range(count):
            left.append(ratio * left[-1] + sums[k, 0:1, :length])
            right.append(ratio * right[-1] + sums[count - 1 - k, 1:2, :length])
        return left[:-1], right[count - 1 :: -1], left[-1], right[-1]

    weight = gain * q_one
    lefts, rights, at_end, at_start = carries(rowsum, rows, chunk)
    coupled = jnp.zeros_like(weight)
    inner = jnp.zeros((1, 128), f32)
    for k in range(rows):
        carry[k, 0:1, :] = lefts[k]
        carry[k, 1:2, :] = rights[k]
        coupled = coupled + lefts[k] * rowsum[k, 1:2, :length] + rights[k] * rowsum[k, 0:1, :length]
        inner = inner + rowsum[k, 0:1, spare]
    colsum[me_c, 0:1, :length] = at_end
    colsum[me_c, 1:2, :length] = at_start
    colsum[me_c, 0:1, spare] = inner + fold(weight * coupled)
    colsum[me_c, 1:2, spare] = jnp.zeros((1, 128), f32)
    mine_c = colsum.at[me_c]
    third = share("col", me_c, cols, lambda to: mine_c, colsum, s3, r3)

    for t in range(rows):
        quads = quadrants(t)
        cos_d, sin_d = f32(mix_cos[t, 0]), f32(mix_sin[t, 0])
        for d in range(1, rows):
            cos_d = jnp.where(me_r == d, f32(mix_cos[t, d]), cos_d)
            sin_d = jnp.where(me_r == d, f32(mix_sin[t, d]), sin_d)
        for j in range(2):
            high, low = split(cos_d * quads[0][j] + sin_d * quads[1][j])
            lanes = slice(t * extent + j * half, t * extent + (j + 1) * half)
            own_hi[:, lanes] = high
            own_lo[:, lanes] = low
    for copy in third:
        copy.wait_recv()

    lefts, rights, at_end, at_start = carries(colsum, cols, group)
    images = 1.0 / (1.0 - whole * whole)
    entry = (at_start + whole * at_end) * images
    exit_ = (at_end + whole * at_start) * images
    for k in range(cols):
        lefts[k] = lefts[k] + entry
        rights[cols - 1 - k] = rights[cols - 1 - k] + exit_
        entry, exit_ = entry * group, exit_ * group
    coupled = jnp.zeros_like(weight)
    inner = jnp.zeros((1, 128), f32)
    left_c, right_c = lefts[0], rights[0]
    for k in range(cols):
        left_c = jnp.where(me_c == k, lefts[k], left_c)
        right_c = jnp.where(me_c == k, rights[k], right_c)
        coupled = coupled + lefts[k] * colsum[k, 1:2, :length] + rights[k] * colsum[k, 0:1, :length]
        inner = inner + colsum[k, 0:1, spare]
    inner = jnp.sum(inner + fold(weight * coupled), axis=1, keepdims=True)
    ratio = inner / previous_ref[...]
    ratio_ref[...] = jnp.broadcast_to(ratio, ratio_ref.shape)
    for k in range(rows):
        carry[k, 0:1, :] = carry[k, 0:1, :] + left_c
        carry[rows - 1 - k, 1:2, :] = carry[rows - 1 - k, 1:2, :] + right_c
        left_c, right_c = left_c * chunk, right_c * chunk

    per = 128 // width
    added = []
    for e in range(0, out_ref.shape[1], 128):
        for k in range(per):
            at = slice(e + k * width, e + (k + 1) * width)
            for t in range(rows):
                lanes = slice(t * extent, (t + 1) * extent)
                r = e // width + k
                high, low = split(
                    from_left[:, lanes] * carry[r, 0:1, lanes]
                    + from_right[:, lanes] * carry[r, 1:2, lanes]
                )
                carried_hi[at, lanes] = high
                carried_lo[at, lanes] = low
        at = slice(e, e + 128)
        added.append(
            lax.dot_general(carried_hi[at, :], own_hi[...], turn, preferred_element_type=f32)
            + lax.dot_general(carried_lo[at, :], own_hi[...], turn, preferred_element_type=f32)
            + lax.dot_general(carried_hi[at, :], own_lo[...], turn, preferred_element_type=f32)
        )
    for copy in fifth:
        copy.wait_recv()
    loads[3].wait()
    stores = []
    for e in range(0, out_ref.shape[1], 128):
        turned = jnp.concatenate([in2[e // width + i] for i in range(per)], axis=0)
        turned = turned + added[e // 128]
        out_ref[:, e : e + 128] = turned.T + ratio * direction_ref[:, e : e + 128]
        copy = pltpu.make_async_copy(
            out_ref.at[:, e : e + 128], out_hbm.at[:, e : e + 128], store_sems.at[e // 128]
        )
        copy.start()
        stores.append(copy)
    for copy in stores:
        copy.wait()
    for copies in (first, second, third, fifth):
        for copy in copies:
            copy.wait_send()


def body(rows, cols, residual, direction, ground_shift, previous):
    extent, here = residual.shape
    width = here // rows
    length = extent * rows
    f32 = jnp.float32
    coarse, fine, eigen = base_tables(extent, rows)
    vmem = pl.BlockSpec(memory_space=pltpu.VMEM)
    smem = pl.BlockSpec(memory_space=pltpu.SMEM)
    dma = pltpu.SemaphoreType.DMA
    per_row, per_col = max(rows - 1, 1), max(cols - 1, 1)
    anywhere = pl.BlockSpec(memory_space=pl.ANY)
    output, ratio = pl.pallas_call(
        functools.partial(kernel, rows, cols),
        out_shape=(
            jax.ShapeDtypeStruct((extent, here), f32),
            jax.ShapeDtypeStruct((1, 1), f32),
        ),
        in_specs=[anywhere, anywhere, anywhere, anywhere, vmem, vmem, vmem],
        out_specs=(anywhere, vmem),
        scratch_shapes=[
            pltpu.VMEM((extent, here), f32),
            pltpu.VMEM((extent, here), f32),
            pltpu.VMEM(coarse.shape, f32),
            pltpu.VMEM(fine.shape, f32),
            pltpu.VMEM((extent, here), f32),
            dma((4,)),
            dma((here // 128,)),
            pltpu.VMEM((rows, width, extent), f32),
            pltpu.VMEM((rows, width, extent), f32),
            pltpu.VMEM((rows, width, extent), f32),
            pltpu.VMEM((rows, width, extent), f32),
            pltpu.VMEM((rows, 2 * extent, extent), jnp.bfloat16),
            pltpu.VMEM((rows, 2 * extent, extent), jnp.bfloat16),
            pltpu.VMEM((width, length), f32),
            pltpu.VMEM((width, length), f32),
            pltpu.VMEM((width, length), f32),
            pltpu.VMEM((extent, length), jnp.bfloat16),
            pltpu.VMEM((extent, length), jnp.bfloat16),
            pltpu.VMEM((here, length), jnp.bfloat16),
            pltpu.VMEM((here, length), jnp.bfloat16),
            pltpu.VMEM((rows, 2, length + 128), f32),
            pltpu.VMEM((cols, 2, length + 128), f32),
            pltpu.VMEM((rows, 2, length), f32),
            dma((per_row,)),
            dma((per_row,)),
            dma((per_row,)),
            dma((per_row,)),
            dma((per_col,)),
            dma((per_col,)),
            dma((per_row,)),
            dma((per_row,)),
        ],
        compiler_params=pltpu.CompilerParams(collective_id=0, has_side_effects=True),
    )(residual, direction, coarse, fine, eigen, ground_shift.reshape(1, 1), previous.reshape(1, 1))
    return output, ratio.reshape(1)


def solution(mesh):
    return jax.shard_map(
        functools.partial(body, mesh.shape["row"], mesh.shape["col"]),
        mesh=mesh,
        in_specs=(P("row", "col"), P("row", "col"), P(), P()),
        out_specs=(P("row", "col"), P()),
        check_vma=False,
    )
```

time: 38.5 us -> 34.2 us (0.89)
  Pallas kernels: 32.4 us -> 28.5 us
  other arithmetic: 2.57 us -> 0 us
  between operations: 1.94 us -> 3.63 us
  local copies, waits for them, and re-layouts: 1.2 us -> 1.87 us
    pallas_call x1, Pallas kernels: 32.4 us -> 28.5 us  [body(): pl.pallas_call(functools.partial(kernel, rows, cols), out_shape=(jax.Shap...]
    add x1 -> x0, other arithmetic: 2.57 us -> none  [body(): return (precond + step_ratio * direction, step_ratio)]
    unnamed x2 -> x1, local copies, waits for them, and re-layouts: 0.01 us -> 1.87 us
    slice x1 -> x0, local copies, waits for them, and re-layouts: 1.19 us -> none  [body(): step_ratio = ratio[0, :1]]
where the time goes in v2:
time: 34.2 us; the launch traced here: 34 us
  Pallas kernels  28.5 us (83%)
  between operations  3.63 us (11%)
  local copies, waits for them, and re-layouts  1.87 us (5%)
    pallas_call x1, Pallas kernels, body(): pl.pallas_call(functools.partial(kernel, rows, cols), out_shape=(jax.Shap...  28.5 us
    unnamed x1, local copies, waits for them, and re-layouts  1.87 us

profile of v2, /device:TPU:0, one launch (start us, length us, event | category | flops | bytes accessed | tf_op | source)
XLA Modules:
  0.0 34.0 jit_solution(10048489684577358140)
XLA Ops:
  1.9 28.5 %shard_map.86 = (f32[256,512]{1,0:T(8,128)}, f32[1,1]{1,0:T(1,128)}) custom-call(f32[256,512]{1,0:T(8,128)} %residual_hbm.1, f32[256,512]{1,0:T(8,128)} %direction_hbm.1, f32[4,256,128]{2,1,0:T(8,128)} %constant.6.clone.coarse_hbm, f32[2,256,128]{2,1,0:T(8,128)} %constant.7.clone.fine_hbm, f32[1,2048]{1,0:T(1,128)} %constant.8.clone.eigen_ref, ...), custom_call_target="tpu_custom_call" | custom-call | tf_op jit(solution)/shard_map/pallas_call | solution.py:402
  30.4 1.9 %copy.13 = f32[256,512]{1,0:T(8,128)} copy(f32[256,512]{1,0:T(8,128)} %get-tuple-element.8) | data formatting | bytes 1048576

commit v3 on v2

--- a/solution.py
+++ b/solution.py
@@ -98,6 +98,7 @@
     own_lo,
     carried_hi,
     carried_lo,
+    added,
     rowsum,
     colsum,
     carry,
@@ -349,21 +350,20 @@
         left_c, right_c = left_c * chunk, right_c * chunk
 
     per = 128 // width
-    added = []
-    for e in range(0, out_ref.shape[1], 128):
-        for k in range(per):
-            at = slice(e + k * width, e + (k + 1) * width)
+    block = out_ref.shape[1]
+    for e in range(0, out_ref.shape[1], block):
+        for r in range(e // width, (e + block) // width):
+            at = slice(r * width, (r + 1) * width)
             for t in range(rows):
                 lanes = slice(t * extent, (t + 1) * extent)
-                r = e // width + k
                 high, low = split(
                     from_left[:, lanes] * carry[r, 0:1, lanes]
                     + from_right[:, lanes] * carry[r, 1:2, lanes]
                 )
                 carried_hi[at, lanes] = high
                 carried_lo[at, lanes] = low
-        at = slice(e, e + 128)
-        added.append(
+        at = slice(e, e + block)
+        added[at, :] = (
             lax.dot_general(carried_hi[at, :], own_hi[...], turn, preferred_element_type=f32)
             + lax.dot_general(carried_lo[at, :], own_hi[...], turn, preferred_element_type=f32)
             + lax.dot_general(carried_hi[at, :], own_lo[...], turn, preferred_element_type=f32)
@@ -374,7 +374,7 @@
     stores = []
     for e in range(0, out_ref.shape[1], 128):
         turned = jnp.concatenate([in2[e // width + i] for i in range(per)], axis=0)
-        turned = turned + added[e // 128]
+        turned = turned + added[e : e + 128, :]
         out_ref[:, e : e + 128] = turned.T + ratio * direction_ref[:, e : e + 128]
         copy = pltpu.make_async_copy(
             out_ref.at[:, e : e + 128], out_hbm.at[:, e : e + 128], store_sems.at[e // 128]
@@ -428,6 +428,7 @@
             pltpu.VMEM((extent, length), jnp.bfloat16),
             pltpu.VMEM((here, length), jnp.bfloat16),
             pltpu.VMEM((here, length), jnp.bfloat16),
+            pltpu.VMEM((here, extent), f32),
             pltpu.VMEM((rows, 2, length + 128), f32),
             pltpu.VMEM((cols, 2, length + 128), f32),
             pltpu.VMEM((rows, 2, length), f32),

time: 34.2 us -> 32.1 us (0.939)
  Pallas kernels: 28.5 us -> 26.4 us
    pallas_call x1, Pallas kernels: 28.5 us -> 26.4 us  [body(): pl.pallas_call(functools.partial(kernel, rows, cols), out_shape=(jax.Shap...]
where the time goes in v3:
time: 32.1 us; the launch traced here: 31.9 us
  Pallas kernels  26.4 us (82%)
  between operations  3.63 us (11%)
  local copies, waits for them, and re-layouts  1.87 us (6%)
    pallas_call x1, Pallas kernels, body(): pl.pallas_call(functools.partial(kernel, rows, cols), out_shape=(jax.Shap...  26.4 us
    unnamed x1, local copies, waits for them, and re-layouts  1.87 us

profile of v3, /device:TPU:0, one launch (start us, length us, event | category | flops | bytes accessed | tf_op | source)
XLA Modules:
  0.0 31.9 jit_solution(7042743739212868865)
XLA Ops:
  1.9 26.4 %shard_map.86 = (f32[256,512]{1,0:T(8,128)}, f32[1,1]{1,0:T(1,128)}) custom-call(f32[256,512]{1,0:T(8,128)} %residual_hbm.1, f32[256,512]{1,0:T(8,128)} %direction_hbm.1, f32[4,256,128]{2,1,0:T(8,128)} %constant.6.clone.coarse_hbm, f32[2,256,128]{2,1,0:T(8,128)} %constant.7.clone.fine_hbm, f32[1,2048]{1,0:T(1,128)} %constant.8.clone.eigen_ref, ...), custom_call_target="tpu_custom_call" | custom-call | tf_op jit(solution)/shard_map/pallas_call | solution.py:402
  28.3 1.9 %copy.13 = f32[256,512]{1,0:T(8,128)} copy(f32[256,512]{1,0:T(8,128)} %get-tuple-element.8) | data formatting | bytes 1048576
